TPU v7x, 512 devices: a whole 4x8x8 slice. The times are simulated.
512 devices in a mesh: trial: 4 (over x), span: 16 (over y, core), heads: 8 (over z).
Axes of the slice: x: 4, y: 8, z: 8, core: 2. Of those that a mesh axis runs over, the one named last changes fastest.
Arguments:
- latents: bfloat16 [64, 4096, 512], P('trial', ('span', 'heads')), parts along dimension 0, may hold values from -6 to 6
- rotary_rows: bfloat16 [64, 4096, 64], P('trial', ('span', 'heads')), parts along dimension 0, may hold values from -6 to 6
- latent_gain: float32 [512], replicated, may hold values from 0.25 to 1.75
- key_up: bfloat16 [2048, 16, 128], P('trial', 'heads'), parts along dimension 0, may hold values from -0.25 to 0.25
- value_up: bfloat16 [2048, 16, 128], P('trial', 'heads'), parts along dimension 0, may hold values from -0.25 to 0.25
Outputs:
- cache_keys: bfloat16 [64, 16, 192, 4096], P(('trial', 'span'), 'heads'), parts along dimension 0
- cache_values: bfloat16 [64, 4096, 16, 128], P(('trial', 'span'), None, 'heads'), parts along dimension 0
There are 4 independent parts, one for each index of `trial`. A program takes and returns all parts, laid end to end along the dimension named above; an argument that names none is the same for every part. Nothing has to cross between parts.
All inputs are finite; a program needn't handle non-finite values.
Results may differ from a plain program's by a relative error of at most 0.0049.
Values may be sent and summed in bfloat16 or wider, within the bound.
A program may use at most 64 MiB of HBM per device.

v0:
```python
import functools

import jax
import jax.numpy as jnp
from jax import lax
from jax.experimental import pallas as pl
from jax.experimental.pallas import tpu as pltpu
from jax.sharding import PartitionSpec as P

MESH = pl.DeviceIdType.MESH


def widen_rows(rows, rotary, key_up, value_up):
    wide_keys = jnp.einsum(
        "btr,rhk->bthk", rows, key_up, preferred_element_type=jnp.float32
    ).astype(jnp.bfloat16)
    shared = jnp.broadcast_to(rotary[:, :, None], wide_keys.shape[:3] + rotary.shape[2:])
    wide_values = jnp.einsum(
        "btr,rhk->bthk", rows, value_up, preferred_element_type=jnp.float32
    ).astype(jnp.bfloat16)
    return (jnp.concatenate([wide_keys, shared], axis=-1), wide_values)


def unit_rows(vectors, row_gain):
    return (
        vectors * lax.rsqrt(jnp.mean(vectors * vectors, axis=-1, keepdims=True) + 1e-06) * row_gain
    )


def plain_shards(latents, rotary_rows, latent_gain, key_up, value_up):
    rows_ready = unit_rows(latents.astype(jnp.float32), latent_gain).astype(jnp.bfloat16)

    def move(block):
        block = lax.all_to_all(block, "span", split_axis=0, concat_axis=1, tiled=True)
        block = block.reshape(block.shape[0], lax.axis_size("span"), -1, block.shape[2])
        block = lax.all_gather(block, "heads", axis=2, tiled=True)
        return block.reshape(block.shape[0], -1, block.shape[3])

    cache_keys, cache_values = widen_rows(move(rows_ready), move(rotary_rows), key_up, value_up)
    return (jnp.transpose(cache_keys, (0, 2, 3, 1)), cache_values)


def sibling(p):
    return p + 1 - 2 * lax.rem(p, 2)


def unit(raw, gain):
    sides, count, depth = raw.shape
    raw = raw.reshape(sides * count, depth).astype(jnp.float32)
    return unit_rows(raw, gain[...]).astype(jnp.bfloat16)


def expand_keys(ready, turned, key_wide, keys):
    heads, turn, count = keys.shape[0], turned.shape[1], turned.shape[2]
    width = keys.shape[1] - turn
    for h in range(heads):
        wide = lax.dot_general(
            key_wide[h * width:(h + 1) * width, :], ready,
            (((1,), (1,)), ((), ())), preferred_element_type=jnp.float32,
        )
        keys[h, :width, :] = wide.astype(jnp.bfloat16)
        for k in range(turned.shape[0]):
            keys[h, width:width + turn, k * count:(k + 1) * count] = turned[k]


def expand_values(ready, value_wide, flat, values):
    both, heads, width = values.shape
    for h in range(0, heads, 2):
        wide = jnp.dot(
            ready, value_wide[:, h * width:(h + 2) * width], preferred_element_type=jnp.float32
        )
        for k in range(2):
            flat[pl.ds(h + k, both, stride=heads), :] = wide[:, k * width:(k + 1) * width]
    values[...] = flat[pl.ds(0, both * heads), :].reshape(both, heads, width).astype(jnp.bfloat16)


def exchange_kernel(
    spans, lat, rot, far_gain, key_up, value_up, keys, values, rows_last, turned_last, key_wide, value_wide, gain,
    rows, turned, raw_key, raw_value, flat, flat_out,
    load_sem, weight_sem, send_sem, recv_sem, pass_sem, land_sem, go_sem,
):
    me, side = lax.axis_index("span"), lax.axis_index("heads")
    other = 1 - side
    count, depth = lat.shape[1], lat.shape[2]
    heads, width = key_up.shape[1], key_up.shape[2]
    value_width = value_up.shape[2]
    turn = rot.shape[1]
    both = 2 * count

    targets, sources = [sibling(me)], [sibling(me)]
    for j in range(1, spans // 2):
        ahead, behind = lax.rem(me + 2 * j, spans), lax.rem(me + spans - 2 * j, spans)
        targets += [ahead, sibling(ahead)]
        sources += [behind, lax.rem(sibling(me) + spans - 2 * j, spans)]
    steps = len(targets)

    barrier = pltpu.get_barrier_semaphore()
    leader = spans - 1
    pl.semaphore_signal(barrier, inc=1, device_id={"heads": other}, device_id_type=MESH)

    @pl.when(me != leader)
    def _():
        pl.semaphore_signal(barrier, inc=1, device_id={"span": leader}, device_id_type=MESH)

    order = list(range(1, steps)) + [0]
    own = (
        pltpu.make_async_copy(lat.at[me], rows.at[me, side], load_sem.at[0]),
        pltpu.make_async_copy(rot.at[me], turned.at[me, side], load_sem.at[1]),
    )
    for copy in own:
        copy.start()
    weights = (
        pltpu.make_async_copy(key_up, raw_key, weight_sem.at[0]),
        pltpu.make_async_copy(value_up, raw_value, weight_sem.at[1]),
        pltpu.make_async_copy(far_gain, gain, weight_sem.at[2]),
    )
    for copy in weights:
        copy.start()

    @pl.when(me == leader)
    def _():
        pl.semaphore_wait(barrier, spans)
        for q in range(spans - 1):
            pl.semaphore_signal(go_sem, inc=1, device_id={"span": q}, device_id_type=MESH)

    @pl.when(me != leader)
    def _():
        pl.semaphore_wait(barrier, 1)

    def forward(q, i):
        made = []
        for k, held in enumerate((rows, turned)):
            made.append(pltpu.make_async_remote_copy(
                src_ref=(lat, rot)[k].at[me] if i == 0 else held.at[q, side], dst_ref=held.at[q, side],
                send_sem=pass_sem.at[k, i], recv_sem=land_sem.at[k, i],
                device_id={"heads": other}, device_id_type=MESH,
            ))
            made[-1].start()
        return made

    passed = [forward(me, 0)]

    @pl.when(me != leader)
    def _():
        pl.semaphore_wait(go_sem, 1)

    sent = {}
    for i in order:
        sent[i] = []
        for k, (held, land) in enumerate(((lat, rows), (rot, turned))):
            sent[i].append(pltpu.make_async_remote_copy(
                src_ref=held.at[targets[i]], dst_ref=land.at[me, side],
                send_sem=send_sem.at[k, i], recv_sem=recv_sem.at[k, i],
                device_id={"span": targets[i]}, device_id_type=MESH,
            ))
            sent[i][-1].start()

    def hear(i):
        for k, (held, land) in enumerate(((lat, rows), (rot, turned))):
            pltpu.make_async_remote_copy(
                src_ref=held.at[targets[i]], dst_ref=land.at[sources[i], side],
                send_sem=send_sem.at[k, i], recv_sem=recv_sem.at[k, i],
                device_id={"span": targets[i]}, device_id_type=MESH,
            ).wait_recv()
        passed.append(forward(sources[i], i + 1))

    def landed(q, i):
        for k, held in enumerate((rows, turned)):
            pltpu.make_async_remote_copy(
                src_ref=held.at[q, other], dst_ref=held.at[q, other],
                send_sem=pass_sem.at[k, i], recv_sem=land_sem.at[k, i],
                device_id={"heads": other}, device_id_type=MESH,
            ).wait_recv()

    def unravel(raw, size, put):
        piece = 128

        @pl.loop(0, depth // piece)
        def _(n):
            r = pl.multiple_of(n * piece, piece)
            part = raw[pl.ds(r, piece)].astype(jnp.float32)
            flat[pl.ds(0, piece * heads), :] = part.reshape(piece * heads, size)
            for h in range(heads):
                put(h, r, piece, flat[pl.ds(h, piece, stride=heads), :])

    def put_value(h, r, piece, block):
        value_wide[pl.ds(r, piece), h * value_width:(h + 1) * value_width] = block.astype(jnp.bfloat16)

    def put_key(h, r, piece, block):
        key_wide[h * width:(h + 1) * width, pl.ds(r, piece)] = block.T.astype(jnp.bfloat16)

    for copy in own:
        copy.wait()
    hear(0)
    for copy in weights:
        copy.wait()
    unravel(raw_key, width, put_key)
    unravel(raw_value, value_width, put_value)
    def finish(q):
        start = pl.multiple_of(q * both, both)
        expand_keys(
            unit(rows[q], gain), turned.at[q], key_wide, keys.at[:, :, pl.ds(start, both)]
        )
        expand_values(
            unit(rows[q], gain), value_wide, flat_out, values.at[pl.ds(start, both)]
        )

    for i in range(1, steps):
        hear(i)
        landed((me, *sources)[i - 1], i - 1)
        finish((me, *sources)[i - 1])
    last = sources[steps - 1]
    start = pl.multiple_of(last * both + side * count, count)
    half = pl.ds(side, 1)
    expand_keys(
        unit(rows[last, half], gain), turned.at[last, half], key_wide,
        keys.at[:, :, pl.ds(start, count)],
    )
    expand_values(
        unit(rows[last, half], gain), value_wide, flat_out, values.at[pl.ds(start, count)]
    )
    landed(sources[steps - 2], steps - 1)
    finish(sources[steps - 2])
    landed(last, steps)
    rows_last[...] = rows[last, pl.ds(other, 1)]
    turned_last[...] = turned[last, pl.ds(other, 1)]
    for pair in (*passed, *sent.values()):
        for copy in pair:
            copy.wait_send()


def write_kernel(
    spans, keys_part, values_part, rows_last, turned_last, key_wide, value_wide, gain,
    keys, values, keys_last, values_last, flat, sem, last_sem,
):
    me, side = lax.axis_index("span"), lax.axis_index("heads")
    count = values_last.shape[0]
    both = 2 * count
    order = [me, sibling(me)]
    for j in range(1, spans // 2):
        behind = lax.rem(me + spans - 2 * j, spans)
        order += [behind, lax.rem(sibling(me) + spans - 2 * j, spans)]
    last = order[-1] * both
    done = [pl.ds(pl.multiple_of(q * both, both), both) for q in order[:-1]]
    done.append(pl.ds(pl.multiple_of(last + side * count, count), count))
    copies = []
    for i, at in enumerate(done):
        copies += [
            pltpu.make_async_copy(keys_part.at[:, :, at], keys.at[0, :, :, at], sem.at[0, i]),
            pltpu.make_async_copy(values_part.at[at], values.at[0, at], sem.at[1, i]),
        ]
    for copy in copies:
        copy.start()
    at = pl.ds(pl.multiple_of(last + (1 - side) * count, count), count)
    ends = (
        pltpu.make_async_copy(keys_last, keys.at[0, :, :, at], last_sem.at[0]),
        pltpu.make_async_copy(values_last, values.at[0, at], last_sem.at[1]),
    )

    @pl.when(me >= 0)
    def _():
        ready = unit(rows_last[...], gain)
        expand_keys(ready, turned_last, key_wide, keys_last)
        ends[0].start()
        expand_values(ready, value_wide, flat, values_last)
        ends[1].start()

    for copy in (*copies, *ends):
        copy.wait()


def shards(latents, rotary_rows, latent_gain, key_up, value_up):
    spans, sides = lax.axis_size("span"), lax.axis_size("heads")
    _, count, depth = latents.shape
    turn = rotary_rows.shape[2]
    heads, width, value_width = key_up.shape[1], key_up.shape[2], value_up.shape[2]
    if (
        latents.shape[0] != spans or spans % 2 or sides != 2 or count % 128 or depth % 128
        or heads % 8 or width != 128 or value_width != 128 or turn % 16
    ):
        return plain_shards(latents, rotary_rows, latent_gain, key_up, value_up)
    length, both = spans * sides * count, sides * count
    steps = spans - 1
    bf16, f32 = jnp.bfloat16, jnp.float32
    near = pl.BlockSpec(memory_space=pltpu.VMEM)
    far = pl.BlockSpec(memory_space=pltpu.HBM)
    args = (latents, jnp.swapaxes(rotary_rows, 1, 2), latent_gain[None], key_up, value_up)
    parts = pl.pallas_call(
        functools.partial(exchange_kernel, spans),
        out_shape=(
            pltpu.VMEM((heads, width + turn, length), bf16),
            pltpu.VMEM((length, heads, value_width), bf16),
            pltpu.VMEM((1, count, depth), bf16),
            pltpu.VMEM((1, turn, count), bf16),
            pltpu.VMEM((heads * width, depth), bf16),
            pltpu.VMEM((depth, heads * value_width), bf16),
            pltpu.VMEM((1, depth), f32),
        ),
        in_specs=[far] * 5,
        out_specs=[near] * 7,
        scratch_shapes=[
            pltpu.VMEM((spans, sides, count, depth), bf16),
            pltpu.VMEM((spans, sides, turn, count), bf16),
            pltpu.VMEM(key_up.shape, bf16),
            pltpu.VMEM(value_up.shape, bf16),
            pltpu.VMEM((128 * heads, 128), f32),
            pltpu.VMEM((both * heads, value_width), f32),
            pltpu.SemaphoreType.DMA((2,)),
            pltpu.SemaphoreType.DMA((3,)),
            pltpu.SemaphoreType.DMA((2, steps)),
            pltpu.SemaphoreType.DMA((2, steps)),
            pltpu.SemaphoreType.DMA((2, spans)),
            pltpu.SemaphoreType.DMA((2, spans)),
            pltpu.SemaphoreType.REGULAR,
        ],
        compiler_params=pltpu.CompilerParams(
            collective_id=0, has_side_effects=True, vmem_limit_bytes=40 * 1024 * 1024
        ),
    )(*(pltpu.with_memory_space_constraint(arg, pltpu.HBM) for arg in args))
    return pl.pallas_call(
        functools.partial(write_kernel, spans),
        out_shape=(
            jax.ShapeDtypeStruct((1, heads, width + turn, length), bf16),
            jax.ShapeDtypeStruct((1, length, heads, value_width), bf16),
        ),
        in_specs=[near] * 7,
        out_specs=[far] * 2,
        scratch_shapes=[
            pltpu.VMEM((heads, width + turn, count), bf16),
            pltpu.VMEM((count, heads, value_width), bf16),
            pltpu.VMEM((count * heads, value_width), f32),
            pltpu.SemaphoreType.DMA((2, spans)),
            pltpu.SemaphoreType.DMA((2,)),
        ],
        compiler_params=pltpu.CompilerParams(vmem_limit_bytes=16 * 1024 * 1024),
    )(*parts)


def solution(mesh):
    return jax.shard_map(
        shards,
        mesh=mesh,
        in_specs=(
            P("trial", ("span", "heads"), None),
            P("trial", ("span", "heads"), None),
            P(),
            P("trial", "heads", None),
            P("trial", "heads", None),
        ),
        out_specs=(
            P(("trial", "span"), "heads", None, None),
            P(("trial", "span"), None, "heads", None),
        ),
        check_vma=False,
    )
```

profile of v0, /device:TPU:1, one launch (start us, length us, event | category | flops | bytes accessed | tf_op | source)
XLA Modules:
  0.0 137.2 jit_solution(3380744454169132950)
XLA Ops:
  7.2 0.0 copy-start
  7.2 0.0 all-gather.4.cloned.1.call-start
  7.2 1.2 fusion.1
  8.5 1.2 fusion.3
  9.7 27.2 %all_to_all.8 = bf16[16,32,512]{2,1,0:T(8,128)(2,1)} all-to-all(bf16[16,32,512]{2,1,0:T(8,128)(2,1)S(1)} %fusion.3), channel_id=1, replica_groups=mesh['trial'=4,'span'=16,'heads'=8] {'span'}, dimensions={0} | all-to-all | bytes 1048576 | tf_op jit(solution)/shard_map/all_to_all | solution.py:34
  37.0 0.0 all-gather.4.cloned.1.call-update
  37.0 1.7 %reshape.51 = bf16[16,2,1024]{2,1,0:T(2,128)(2,1)} reshape(bf16[16,32,64]{2,1,0:T(8,128)(2,1)} %param.6) | data formatting | bytes 131072
  38.7 3.4 %all-to-all-start.1 = ((bf16[16,2,1024]{2,1,0:T(2,128)(2,1)}), bf16[16,2,1024]{2,1,0:T(2,128)(2,1)S(1)}, u32[]{:S(2)}, u32[]{:S(2)}) async-start(bf16[16,2,1024]{2,1,0:T(2,128)(2,1)} %reshape.51), calls=%async_computation.1 | async-start | bytes 131072 | tf_op jit(solution)/shard_map/all_to_all | solution.py:34
  42.1 1.1 copy.7
  43.2 6.1 %all-to-all-done.1 = bf16[16,2,1024]{2,1,0:T(2,128)(2,1)S(1)} async-done(((bf16[16,2,1024]{2,1,0:T(2,128)(2,1)}), bf16[16,2,1024]{2,1,0:T(2,128)(2,1)S(1)}, u32[]{:S(2)}, u32[]{:S(2)}) %all-to-all-start.1) | async-done | bytes 65568 | tf_op jit(solution)/shard_map/all_to_all | solution.py:34
  49.3 0.1 reshape.52
  49.4 33.0 %all-gather.1 = bf16[16,256,64]{2,1,0:T(8,128)(2,1)S(1)} all-gather(bf16[16,32,64]{2,1,0:T(8,128)(2,1)S(1)} %reshape.52), channel_id=3, replica_groups=mesh['trial'=4,'span'=16,'heads'=8] {'heads'}, dimensions={1}, use_global_device_ids=true | all-gather | bytes 589824 | tf_op jit(solution)/shard_map/all_gather | solution.py:36
  82.5 0.3 copy.8
  82.8 20.5 %all-gather.4.cloned.1.call-done = bf16[16,256,512]{2,1,0:T(8,128)(2,1)} async-done(((bf16[16,32,512]{2,1,0:T(8,128)(2,1)}), bf16[16,256,512]{2,1,0:T(8,128)(2,1)}) %all-gather.4.cloned.1.call-update) | async-done | bytes 4194320 | tf_op jit(solution)/shard_map/all_gather | solution.py:36
  103.3 3.5 %fusion.5 = f32[4096,256]{0,1:S(1)} fusion(bf16[4096,512]{1,0:T(8,128)(2,1)} %bitcast.16, bf16[512,256]{0,1:T(8,128)(2,1)S(1)} %bitcast.19), kind=kOutput, calls=%fused_computation.11 | convolution fusion | flops 1073741824 | bytes 8650752
  106.8 0.0 copy-start.1
  106.8 0.3 convert_bitcast_fusion
  107.1 0.0 copy-done
  107.1 1.9 %copy-done.1 = bf16[16,256,512]{2,1,0:T(8,128)(2,1)S(1)} copy-done((bf16[16,256,512]{2,1,0:T(8,128)(2,1)S(1)}, bf16[16,256,512]{2,1,0:T(8,128)(2,1)}, u32[]{:S(2)}) %copy-start.1) | copy-done | bytes 4194328
  109.0 1.3 fusion
  110.3 18.1 %copy.10 = bf16[1,4096,2,128]{3,2,1,0:T(2,128)(2,1)} copy(bf16[1,4096,2,128]{3,1,2,0:T(8,128)(2,1)S(1)} %fusion) | data formatting | bytes 4194304
  128.4 0.1 broadcast_in_dim.10
  128.5 1.9 %maximum_bitcast_fusion = bf16[1,2,192,4096]{3,2,1,0:T(8,128)(2,1)} fusion(bf16[1,4096,2,64]{1,3,2,0:T(8,128)(2,1)S(1)} %broadcast_in_dim.10, bf16[1,4096,2,128]{1,3,2,0:T(8,128)(2,1)S(1)} %convert_bitcast_fusion), kind=kLoop, calls=%fused_computation.2 | loop fusion | flops 6291456 | bytes 6291456 | tf_op jit(solution)/shard_map/transpose | solution.py:40
  (1 shorter events, 0.0 us)
Async XLA Ops:
  7.2 99.9 %copy-start = (bf16[512,2,128]{2,1,0:T(2,128)(2,1)S(1)}, bf16[512,2,128]{2,1,0:T(2,128)(2,1)}, u32[]{:S(2)}) copy-start(bf16[512,2,128]{2,1,0:T(2,128)(2,1)} %param.9) | copy-start | bytes 786436
  7.2 96.2 %all-gather.4.cloned.1.call-start = ((), (), s32[]{:S(2)}) async-start(), calls=%async_computation.2 | async-start | bytes 4718592 | tf_op jit(solution)/shard_map/all_gather | solution.py:36
  38.7 10.6 %all-to-all-start.1 = ((bf16[16,2,1024]{2,1,0:T(2,128)(2,1)}), bf16[16,2,1024]{2,1,0:T(2,128)(2,1)S(1)}, u32[]{:S(2)}, u32[]{:S(2)}) async-start(bf16[16,2,1024]{2,1,0:T(2,128)(2,1)} %reshape.51), calls=%async_computation.1 | async-start | bytes 131072 | tf_op jit(solution)/shard_map/all_to_all | solution.py:34
  106.8 2.2 %copy-start.1 = (bf16[16,256,512]{2,1,0:T(8,128)(2,1)S(1)}, bf16[16,256,512]{2,1,0:T(8,128)(2,1)}, u32[]{:S(2)}) copy-start(bf16[16,256,512]{2,1,0:T(8,128)(2,1)} %all-gather.4.cloned.1.call-done) | copy-start | bytes 12582916
Sparse Core Ops, SparseCore 0:
  37.1 66.1 all-gather.3
where the time goes:
time: 138 us; the launch traced here: 137 us
  blocking collectives  60.3 us (44%)
  waiting for transfers between devices  26.6 us (19%)
  local copies, waits for them, and re-layouts  23.4 us (17%)
  between operations  14.1 us (10%)
  matrix products  4.72 us (3%)
  other arithmetic  4.63 us (3%)
  starting transfers between devices  3.44 us (2%)
    all_gather x1, blocking collectives, move(): block = lax.all_gather(block, 'heads', axis=2, tiled=True)  33 us
    all_to_all x1, blocking collectives, move(): lax.all_to_all(block, 'span', split_axis=0, concat_axis=1, tiled=True)  27.2 us
    unnamed x8, local copies, waits for them, and re-layouts  22.9 us
    all_gather x1, waiting for transfers between devices, move(): block = lax.all_gather(block, 'heads', axis=2, tiled=True)  20.5 us
    all_to_all x1, waiting for transfers between devices, move(): lax.all_to_all(block, 'span', split_axis=0, concat_axis=1, tiled=True)  6.09 us
    unnamed x1, matrix products  3.47 us
    all_to_all x1, starting transfers between devices, move(): lax.all_to_all(block, 'span', split_axis=0, concat_axis=1, tiled=True)  3.4 us
  transfers between devices with their start and end apart: 2, of which 2 were waited for; matrix products, arithmetic and copies ran while one was open for 2% of the time, Pallas kernels for 0%

commit v1 on v0

v1 whole, which is shorter than its diff:
```python
import functools

import jax
import jax.numpy as jnp
from jax import lax
from jax.experimental import pallas as pl
from jax.experimental.pallas import tpu as pltpu
from jax.sharding import PartitionSpec as P

MESH = pl.DeviceIdType.MESH
BF16, F32 = jnp.bfloat16, jnp.float32

SPANS, RING = 16, 8
COUNT, DEPTH = 32, 512
TURN, WIDTH = 64, 128
TILES = 8
BATCH = 4


def widen_rows(rows, rotary, key_up, value_up):
    wide_keys = jnp.einsum(
        "btr,rhk->bthk", rows, key_up, preferred_element_type=jnp.float32
    ).astype(jnp.bfloat16)
    shared = jnp.broadcast_to(rotary[:, :, None], wide_keys.shape[:3] + rotary.shape[2:])
    wide_values = jnp.einsum(
        "btr,rhk->bthk", rows, value_up, preferred_element_type=jnp.float32
    ).astype(jnp.bfloat16)
    return (jnp.concatenate([wide_keys, shared], axis=-1), wide_values)


def unit_rows(vectors, row_gain):
    return (
        vectors * lax.rsqrt(jnp.mean(vectors * vectors, axis=-1, keepdims=True) + 1e-06) * row_gain
    )


def plain_shards(latents, rotary_rows, latent_gain, key_up, value_up):
    rows_ready = unit_rows(latents.astype(jnp.float32), latent_gain).astype(jnp.bfloat16)

    def move(block):
        block = lax.all_to_all(block, "span", split_axis=0, concat_axis=1, tiled=True)
        block = block.reshape(block.shape[0], lax.axis_size("span"), -1, block.shape[2])
        block = lax.all_gather(block, "heads", axis=2, tiled=True)
        return block.reshape(block.shape[0], -1, block.shape[3])

    cache_keys, cache_values = widen_rows(move(rows_ready), move(rotary_rows), key_up, value_up)
    return (jnp.transpose(cache_keys, (0, 2, 3, 1)), cache_values)


def source(me, k):
    j, flip = k // 2, k % 2
    away = ((j + 1) // 2) * (2 * (j % 2) - 1)
    core = (me % 2) * (1 - 2 * flip) + flip
    return ((me // 2 + away + SPANS // 2) % (SPANS // 2)) * 2 + core


def target(me, k):
    j, flip = k // 2, k % 2
    away = ((j + 1) // 2) * (2 * (j % 2) - 1)
    core = (me % 2) * (1 - 2 * flip) + flip
    return ((me // 2 - away + SPANS // 2) % (SPANS // 2)) * 2 + core


def exchange_kernel(
    lat, rot, far_gain, key_up, value_up, keys, values,
    buf, stage, rot_raw, raw_w, key_wide, value_wide, gain, pick, flat,
    load_sem, y_send, y_recv, z_send, z_recv,
):
    me, z = lax.axis_index("span"), lax.axis_index("heads")
    ahead, behind = lax.rem(z + 1, RING), lax.rem(z + RING - 1, RING)

    barrier = pltpu.get_barrier_semaphore()
    for near in (ahead, behind):
        pl.semaphore_signal(barrier, inc=1, device_id={"heads": near}, device_id_type=MESH)
    for k in range(1, SPANS):
        pl.semaphore_signal(barrier, inc=1, device_id={"span": target(me, k)}, device_id_type=MESH)

    rot_load = pltpu.make_async_copy(rot, rot_raw, load_sem.at[0])
    rot_load.start()
    loads = []
    for t in range(TILES):
        rows = pl.ds(16 * (t // 4), 16)
        columns = pl.ds(128 * (t % 4), 128)
        loads.append(pltpu.make_async_copy(
            lat.at[:, rows, columns], stage.at[:, t], load_sem.at[1 + t]
        ))
    weights = [
        pltpu.make_async_copy(key_up, raw_w.at[0], load_sem.at[9]),
        pltpu.make_async_copy(value_up, raw_w.at[1], load_sem.at[10]),
        pltpu.make_async_copy(far_gain, gain, load_sem.at[11]),
    ]
    for copy in (*loads, *weights):
        copy.start()
    rot_load.wait()

    @pl.loop(0, SPANS)
    def _(s):
        part = rot_raw[s].astype(F32)
        stage[s, TILES] = jnp.concatenate([part[:16], part[16:]], axis=1).astype(BF16)

    for copy in loads:
        copy.wait()
    pl.semaphore_wait(barrier, SPANS + 1)

    def z_copy(way, d, k):
        if way == 0:
            here, there, to = (RING + 1 - d) % RING, RING - d, ahead
        else:
            here, there, to = d - 1, d, behind
        src = stage.at[me] if (d == 1 and k == 0) else buf.at[here, k]
        n = (way * 4 + d - 1) * SPANS + k
        return pltpu.make_async_remote_copy(
            src_ref=src, dst_ref=buf.at[there, k], send_sem=z_send.at[n], recv_sem=z_recv.at[n],
            device_id={"heads": to}, device_id_type=MESH,
        )

    def y_copy(k):
        to = target(me, k)
        return pltpu.make_async_remote_copy(
            src_ref=stage.at[to], dst_ref=buf.at[0, k], send_sem=y_send.at[k], recv_sem=y_recv.at[k],
            device_id={"span": to}, device_id_type=MESH,
        )

    heard = set()

    def need(way, d, k):
        if d == 0:
            if k and (0, k) not in heard:
                heard.add((0, k))
                y_copy(k).wait_recv()
        elif (way, d, k) not in heard:
            heard.add((way, d, k))
            z_copy(way, d, k).wait_recv()

    def last_way(k):
        return k % 2

    sent = []

    def forward(d, ks):
        for k in ks:
            for way in (0, 1):
                need(way, d - 1, k)
                if d < 4 or way == last_way(k):
                    z_copy(way, d, k).start()
                    sent.append((way, d, k))

    forward(1, [0])
    for k in range(1, SPANS):
        y_copy(k).start()
    buf[0, 0] = stage[me]

    for copy in weights:
        copy.wait()
    for w, put in ((0, key_wide), (1, value_wide)):
        @pl.loop(0, 4)
        def _(n):
            r = pl.multiple_of(n * 256, 256)
            flat[...] = raw_w[w, pl.ds(r, 256), :].astype(F32)
            at = pl.multiple_of(n * 128, 128)
            for h in range(2):
                block = flat[pl.ds(h, 128, stride=2), :]
                if w == 0:
                    key_wide[h * WIDTH:(h + 1) * WIDTH, pl.ds(at, 128)] = block.T.astype(BF16)
                else:
                    value_wide[pl.ds(at, 128), h * WIDTH:(h + 1) * WIDTH] = block.astype(BF16)
    row = lax.broadcasted_iota(jnp.int32, (64, 128), 0)
    column = lax.broadcasted_iota(jnp.int32, (64, 128), 1)
    for half in range(2):
        place = (row // 16) * 32 + half * 16 + row % 16
        pick[half] = jnp.where(place == column, 1.0, 0.0).astype(BF16)

    def expand(k, other):
        group = z // 4 if not other else 1 - z // 4
        start = pl.multiple_of(source(me, k) * 256 + group * 128, 128)
        rows, turned = [], []
        for zz in range(4):
            rel = lax.rem(group * 4 + zz + RING - z, RING)
            for half in range(2):
                raw = jnp.concatenate(
                    [buf[rel, k, half * 4 + c].astype(F32) for c in range(4)], axis=1
                )
                rows.append(unit_rows(raw, gain[...]).astype(BF16))
            turned.append(buf[rel, k, TILES])
        ready = jnp.concatenate(rows, axis=0)
        turned = jnp.concatenate(turned, axis=0)
        wide = lax.dot_general(
            key_wide[...], ready, (((1,), (1,)), ((), ())), preferred_element_type=F32
        ).astype(BF16)
        halves = [
            lax.dot_general(turned, pick[half], (((0,), (0,)), ((), ())), preferred_element_type=F32)
            for half in range(2)
        ]
        shared = (halves[0][:TURN] + halves[1][TURN:]).astype(BF16)
        for h in range(2):
            keys[h, :WIDTH, pl.ds(start, 128)] = wide[h * WIDTH:(h + 1) * WIDTH]
            keys[h, WIDTH:, pl.ds(start, 128)] = shared
        wide = jnp.dot(ready, value_wide[...], preferred_element_type=F32)
        for h in range(2):
            flat[pl.ds(h, 128, stride=2), :] = wide[:, h * WIDTH:(h + 1) * WIDTH]
        values[pl.ds(pl.multiple_of(start * 2, 256), 256), :] = flat[...].astype(BF16)

    def compute(other, b):
        ks = batch(b)
        for k in ks:
            for way in (0, 1):
                need(way, 3, k)
            if other:
                need(last_way(k), 4, k)
        for k in ks:
            assert (0, k) in heard or k == 0

        @pl.loop(ks[0], ks[-1] + 1)
        def _(k):
            expand(k, other)

    def batch(b):
        return list(range(b * BATCH, (b + 1) * BATCH))

    forward(1, batch(0)[1:])
    forward(1, batch(1))
    forward(2, batch(0))
    forward(1, batch(2))
    forward(2, batch(1))
    forward(3, batch(0))
    forward(1, batch(3))
    forward(2, batch(2))
    forward(4, batch(0))
    forward(3, batch(1))
    compute(False, 0)
    forward(2, batch(3))
    compute(True, 0)
    forward(4, batch(1))
    forward(3, batch(2))
    compute(False, 1)
    forward(3, batch(3))
    compute(True, 1)
    forward(4, batch(2))
    compute(False, 2)
    forward(4, batch(3))
    compute(False, 3)
    compute(True, 2)
    compute(True, 3)

    for k in range(1, SPANS):
        y_copy(k).wait_send()
    for way, d, k in sent:
        z_copy(way, d, k).wait_send()


def write_kernel(keys_part, values_part, keys, values, sem):
    copies = []
    for h in range(2):
        for n in range(2):
            rows = pl.ds(96 * n, 96)
            copies.append(pltpu.make_async_copy(
                keys_part.at[h, rows], keys.at[0, h, rows], sem.at[len(copies)]
            ))
    for n in range(4):
        rows = pl.ds(2048 * n, 2048)
        copies.append(pltpu.make_async_copy(
            values_part.at[rows], values.at[rows], sem.at[len(copies)]
        ))
    for copy in copies:
        copy.start()
    for copy in copies:
        copy.wait()


def shards(latents, rotary_rows, latent_gain, key_up, value_up):
    shape = (lax.axis_size("span"), lax.axis_size("heads"), *latents.shape, rotary_rows.shape[2])
    if shape != (SPANS, RING, SPANS, COUNT, DEPTH, TURN) or key_up.shape != (DEPTH, 2, WIDTH) or (
        value_up.shape != (DEPTH, 2, WIDTH)
    ):
        return plain_shards(latents, rotary_rows, latent_gain, key_up, value_up)
    length = SPANS * RING * COUNT
    near = pl.BlockSpec(memory_space=pltpu.VMEM)
    far = pl.BlockSpec(memory_space=pltpu.HBM)
    args = (
        latents, rotary_rows, latent_gain[None],
        key_up.reshape(2 * DEPTH, WIDTH), value_up.reshape(2 * DEPTH, WIDTH),
    )
    parts = pl.pallas_call(
        exchange_kernel,
        out_shape=(
            pltpu.VMEM((2, WIDTH + TURN, length), BF16),
            pltpu.VMEM((2 * length, WIDTH), BF16),
        ),
        in_specs=[far] * 5,
        out_specs=[near] * 2,
        scratch_shapes=[
            pltpu.VMEM((RING, SPANS, TILES + 1, 16, 128), BF16),
            pltpu.VMEM((SPANS, TILES + 1, 16, 128), BF16),
            pltpu.VMEM((SPANS, COUNT, TURN), BF16),
            pltpu.VMEM((2, 2 * DEPTH, WIDTH), BF16),
            pltpu.VMEM((2 * WIDTH, DEPTH), BF16),
            pltpu.VMEM((DEPTH, 2 * WIDTH), BF16),
            pltpu.VMEM((1, DEPTH), F32),
            pltpu.VMEM((2, 64, 128), BF16),
            pltpu.VMEM((256, WIDTH), F32),
            pltpu.SemaphoreType.DMA((12,)),
            pltpu.SemaphoreType.DMA((SPANS,)),
            pltpu.SemaphoreType.DMA((SPANS,)),
            pltpu.SemaphoreType.DMA((8 * SPANS,)),
            pltpu.SemaphoreType.DMA((8 * SPANS,)),
        ],
        compiler_params=pltpu.CompilerParams(
            collective_id=0, has_side_effects=True, vmem_limit_bytes=40 * 1024 * 1024
        ),
    )(*(pltpu.with_memory_space_constraint(arg, pltpu.HBM) for arg in args))
    keys, values = pl.pallas_call(
        write_kernel,
        out_shape=(
            jax.ShapeDtypeStruct((1, 2, WIDTH + TURN, length), BF16),
            jax.ShapeDtypeStruct((2 * length, WIDTH), BF16),
        ),
        in_specs=[near] * 2,
        out_specs=[far] * 2,
        scratch_shapes=[pltpu.SemaphoreType.DMA((8,))],
        compiler_params=pltpu.CompilerParams(vmem_limit_bytes=16 * 1024 * 1024),
    )(*parts)
    return keys, values.reshape(1, length, 2, WIDTH)


def solution(mesh):
    return jax.shard_map(
        shards,
        mesh=mesh,
        in_specs=(
            P("trial", ("span", "heads"), None),
            P("trial", ("span", "heads"), None),
            P(),
            P("trial", "heads", None),
            P("trial", "heads", None),
        ),
        out_specs=(
            P(("trial", "span"), "heads", None, None),
            P(("trial", "span"), None, "heads", None),
        ),
        check_vma=False,
    )
```

time: 138 us -> 73 us (0.53)
  Pallas kernels: 0 us -> 72.3 us
  blocking collectives: 60.3 us -> 0 us
  waiting for transfers between devices: 26.6 us -> 0 us
  local copies, waits for them, and re-layouts: 23.4 us -> 0 us
  between operations: 14.1 us -> 0.64 us
  matrix products: 4.72 us -> 0 us
  other arithmetic: 4.63 us -> 0 us
  starting transfers between devices: 3.44 us -> 0 us
    pallas_call x0 -> x2, Pallas kernels: none -> 72.3 us  [the longest x1 69.9 us: shards(): pl.pallas_call(exchange_kernel, out_shape=(pltpu.VMEM((2, WIDTH + TURN, l...]
    all_gather x1 -> x0, blocking collectives: 33 us -> none  [move(): block = lax.all_gather(block, 'heads', axis=2, tiled=True)]
    all_to_all x1 -> x0, blocking collectives: 27.2 us -> none  [move(): lax.all_to_all(block, 'span', split_axis=0, concat_axis=1, tiled=True)]
    unnamed x8 -> x0, local copies, waits for them, and re-layouts: 22.9 us -> none
    all_gather x1 -> x0, waiting for transfers between devices: 20.5 us -> none  [move(): block = lax.all_gather(block, 'heads', axis=2, tiled=True)]
    all_to_all x1 -> x0, waiting for transfers between devices: 6.09 us -> none  [move(): lax.all_to_all(block, 'span', split_axis=0, concat_axis=1, tiled=True)]
    unnamed x1 -> x0, matrix products: 3.47 us -> none
    all_to_all x1 -> x0, starting transfers between devices: 3.4 us -> none  [move(): lax.all_to_all(block, 'span', split_axis=0, concat_axis=1, tiled=True)]
  transfers between devices with their start and end apart: 2 -> 0, of which waited for: 2 -> 0; matrix products, arithmetic and copies ran while one was open for 2% -> 0% of each run, Pallas kernels for 0% -> 0%
where the time goes in v1:
time: 73 us; the launch traced here: 72.9 us
  Pallas kernels  72.3 us (99%)
    pallas_call x1, Pallas kernels, shards(): pl.pallas_call(exchange_kernel, out_shape=(pltpu.VMEM((2, WIDTH + TURN, l...  69.9 us
    pallas_call x1, Pallas kernels, shards(): pl.pallas_call(write_kernel, out_shape=(jax.ShapeDtypeStruct((1, 2, WIDTH...  2.4 us

profile of v1, /device:TPU:1, one launch (start us, length us, event | category | flops | bytes accessed | tf_op | source)
XLA Modules:
  0.0 72.9 jit_solution(1240258901610700226)
XLA Ops:
  0.6 69.9 %shard_map.68 = (bf16[2,192,4096]{2,1,0:T(8,128)(2,1)S(1)}, bf16[8192,128]{1,0:T(8,128)(2,1)S(1)}) custom-call(bf16[16,32,512]{2,1,0:T(8,128)(2,1)} %lat.1, bf16[16,32,64]{2,1,0:T(8,128)(2,1)} %rot.1, f32[1,512]{1,0:T(1,128)} %bitcast.6, bf16[1024,128]{1,0:T(8,128)(2,1)} %bitcast.4, bf16[1024,128]{1,0:T(8,128)(2,1)} %bitcast.5), custom_call_target="tpu_custom_call" | custom-call | tf_op jit(solution)/shard_map/pallas_call | solution.py:283
  70.5 2.4 %shard_map.69 = (bf16[1,2,192,4096]{3,2,1,0:T(8,128)(2,1)}, bf16[8192,128]{1,0:T(8,128)(2,1)}) custom-call(bf16[2,192,4096]{2,1,0:T(8,128)(2,1)S(1)} %get-tuple-element.6.keys_part, bf16[8192,128]{1,0:T(8,128)(2,1)S(1)} %get-tuple-element.7.values_part), custom_call_target="tpu_custom_call" | custom-call | tf_op jit(solution)/shard_map/pallas_call | solution.py:311

commit v2 on v1

--- a/solution.py
+++ b/solution.py
@@ -14,7 +14,6 @@
 COUNT, DEPTH = 32, 512
 TURN, WIDTH = 64, 128
 TILES = 8
-BATCH = 4
 
 
 def widen_rows(rows, rotary, key_up, value_up):
@@ -64,16 +63,18 @@
 def exchange_kernel(
     lat, rot, far_gain, key_up, value_up, keys, values,
     buf, stage, rot_raw, raw_w, key_wide, value_wide, gain, pick, flat,
-    load_sem, y_send, y_recv, z_send, z_recv,
+    ready, load_sem, y_send, y_recv, z_send, z_recv,
 ):
     me, z = lax.axis_index("span"), lax.axis_index("heads")
     ahead, behind = lax.rem(z + 1, RING), lax.rem(z + RING - 1, RING)
 
     barrier = pltpu.get_barrier_semaphore()
-    for near in (ahead, behind):
-        pl.semaphore_signal(barrier, inc=1, device_id={"heads": near}, device_id_type=MESH)
-    for k in range(1, SPANS):
-        pl.semaphore_signal(barrier, inc=1, device_id={"span": target(me, k)}, device_id_type=MESH)
+    sibling = target(me, 1)
+    greeted = [{"heads": ahead}, {"heads": behind}, {"span": sibling}]
+    greeted += [{"span": sibling, "heads": ahead}, {"span": sibling, "heads": behind}]
+    greeted += [{"span": target(me, k)} for k in range(2, 6)]
+    for near in greeted:
+        pl.semaphore_signal(barrier, inc=1, device_id=near, device_id_type=MESH)
 
     rot_load = pltpu.make_async_copy(rot, rot_raw, load_sem.at[0])
     rot_load.start()
@@ -100,18 +101,22 @@
 
     for copy in loads:
         copy.wait()
-    pl.semaphore_wait(barrier, SPANS + 1)
+    pl.semaphore_wait(barrier, len(greeted))
 
     def z_copy(way, d, k):
         if way == 0:
             here, there, to = (RING + 1 - d) % RING, RING - d, ahead
         else:
             here, there, to = d - 1, d, behind
-        src = stage.at[me] if (d == 1 and k == 0) else buf.at[here, k]
+        src, device = buf.at[here, k], {"heads": to}
+        if d == 1 and k == 0:
+            src = stage.at[me]
+        if d == 1 and k == 1:
+            src, device = stage.at[sibling], {"span": sibling, "heads": to}
         n = (way * 4 + d - 1) * SPANS + k
         return pltpu.make_async_remote_copy(
             src_ref=src, dst_ref=buf.at[there, k], send_sem=z_send.at[n], recv_sem=z_recv.at[n],
-            device_id={"heads": to}, device_id_type=MESH,
+            device_id=device, device_id_type=MESH,
         )
 
     def y_copy(k):
@@ -140,14 +145,18 @@
     def forward(d, ks):
         for k in ks:
             for way in (0, 1):
-                need(way, d - 1, k)
+                if d > 1 or k > 1:
+                    need(way, d - 1, k)
                 if d < 4 or way == last_way(k):
                     z_copy(way, d, k).start()
                     sent.append((way, d, k))
 
-    forward(1, [0])
-    for k in range(1, SPANS):
-        y_copy(k).start()
+    def spread(ks):
+        for k in ks:
+            y_copy(k).start()
+
+    forward(1, [0, 1])
+    spread(range(1, 6))
     buf[0, 0] = stage[me]
 
     for copy in weights:
@@ -156,7 +165,7 @@
         @pl.loop(0, 4)
         def _(n):
             r = pl.multiple_of(n * 256, 256)
-            flat[...] = raw_w[w, pl.ds(r, 256), :].astype(F32)
+            flat[pl.ds(0, 256), :] = raw_w[w, pl.ds(r, 256), :].astype(F32)
             at = pl.multiple_of(n * 128, 128)
             for h in range(2):
                 block = flat[pl.ds(h, 128, stride=2), :]
@@ -170,81 +179,107 @@
         place = (row // 16) * 32 + half * 16 + row % 16
         pick[half] = jnp.where(place == column, 1.0, 0.0).astype(BF16)
 
-    def expand(k, other):
+    def expand(p, other):
         group = z // 4 if not other else 1 - z // 4
-        start = pl.multiple_of(source(me, k) * 256 + group * 128, 128)
-        rows, turned = [], []
-        for zz in range(4):
-            rel = lax.rem(group * 4 + zz + RING - z, RING)
-            for half in range(2):
-                raw = jnp.concatenate(
-                    [buf[rel, k, half * 4 + c].astype(F32) for c in range(4)], axis=1
-                )
-                rows.append(unit_rows(raw, gain[...]).astype(BF16))
-            turned.append(buf[rel, k, TILES])
-        ready = jnp.concatenate(rows, axis=0)
-        turned = jnp.concatenate(turned, axis=0)
-        wide = lax.dot_general(
-            key_wide[...], ready, (((1,), (1,)), ((), ())), preferred_element_type=F32
-        ).astype(BF16)
-        halves = [
-            lax.dot_general(turned, pick[half], (((0,), (0,)), ((), ())), preferred_element_type=F32)
-            for half in range(2)
-        ]
-        shared = (halves[0][:TURN] + halves[1][TURN:]).astype(BF16)
-        for h in range(2):
-            keys[h, :WIDTH, pl.ds(start, 128)] = wide[h * WIDTH:(h + 1) * WIDTH]
-            keys[h, WIDTH:, pl.ds(start, 128)] = shared
-        wide = jnp.dot(ready, value_wide[...], preferred_element_type=F32)
-        for h in range(2):
-            flat[pl.ds(h, 128, stride=2), :] = wide[:, h * WIDTH:(h + 1) * WIDTH]
-        values[pl.ds(pl.multiple_of(start * 2, 256), 256), :] = flat[...].astype(BF16)
-
-    def compute(other, b):
-        ks = batch(b)
-        for k in ks:
+        pair = (2 * p, 2 * p + 1)
+        for k in pair:
+            need(0, 0, k)
             for way in (0, 1):
                 need(way, 3, k)
             if other:
                 need(last_way(k), 4, k)
-        for k in ks:
-            assert (0, k) in heard or k == 0
-
-        @pl.loop(ks[0], ks[-1] + 1)
-        def _(k):
-            expand(k, other)
-
-    def batch(b):
-        return list(range(b * BATCH, (b + 1) * BATCH))
-
-    forward(1, batch(0)[1:])
-    forward(1, batch(1))
-    forward(2, batch(0))
-    forward(1, batch(2))
-    forward(2, batch(1))
-    forward(3, batch(0))
-    forward(1, batch(3))
-    forward(2, batch(2))
-    forward(4, batch(0))
-    forward(3, batch(1))
-    compute(False, 0)
-    forward(2, batch(3))
-    compute(True, 0)
-    forward(4, batch(1))
-    forward(3, batch(2))
-    compute(False, 1)
-    forward(3, batch(3))
-    compute(True, 1)
-    forward(4, batch(2))
-    compute(False, 2)
-    forward(4, batch(3))
-    compute(False, 3)
-    compute(True, 2)
-    compute(True, 3)
-
+        rels = [lax.rem(group * 4 + zz + RING - z, RING) for zz in range(4)]
+        starts = [pl.multiple_of(source(me, k) * 256 + group * 128, 128) for k in pair]
+        for i, k in enumerate(pair):
+            for zz in range(4):
+                for half in range(2):
+                    raw = jnp.concatenate(
+                        [buf[rels[zz], k, half * 4 + c].astype(F32) for c in range(4)], axis=1
+                    )
+                    ready[pl.ds(i * 128 + zz * 32 + half * 16, 16), :] = (
+                        unit_rows(raw, gain[...]).astype(BF16)
+                    )
+        wide = lax.dot_general(
+            key_wide[...], ready[...], (((1,), (1,)), ((), ())), preferred_element_type=F32
+        ).astype(BF16)
+        for i, k in enumerate(pair):
+            turned = jnp.concatenate([buf[rels[zz], k, TILES] for zz in range(4)], axis=0)
+            halves = [
+                lax.dot_general(
+                    turned, pick[half], (((0,), (0,)), ((), ())), preferred_element_type=F32
+                )
+                for half in range(2)
+            ]
+            shared = (halves[0][:TURN] + halves[1][TURN:]).astype(BF16)
+            for h in range(2):
+                keys[h, :WIDTH, pl.ds(starts[i], 128)] = (
+                    wide[h * WIDTH:(h + 1) * WIDTH, i * 128:(i + 1) * 128]
+                )
+                keys[h, WIDTH:, pl.ds(starts[i], 128)] = shared
+        wide = jnp.dot(ready[...], value_wide[...], preferred_element_type=F32)
+        for h in range(2):
+            flat[pl.ds(h, 256, stride=2), :] = wide[:, h * WIDTH:(h + 1) * WIDTH]
+        for i in range(2):
+            at = pl.multiple_of(starts[i] * 2, 256)
+            values[pl.ds(at, 256), :] = flat[pl.ds(i * 256, 256), :].astype(BF16)
+
+    def hop(d, *pairs):
+        for p in pairs:
+            forward(d, [2 * p, 2 * p + 1])
+
+    own, far = functools.partial(expand, other=False), functools.partial(expand, other=True)
+
+    forward(2, [0])
+    forward(1, [2])
+    forward(2, [1])
+    forward(1, [3, 4, 5])
+    spread(range(6, 10))
+    hop(2, 1)
+    hop(1, 3, 4)
+    spread(range(10, 16))
+    hop(2, 2)
+    hop(3, 0)
+    hop(2, 3)
+    hop(3, 1)
+    hop(1, 5)
+    hop(2, 4)
+    hop(1, 6)
+    hop(4, 0)
+    own(0)
+    hop(3, 2)
+    hop(1, 7)
+    own(1)
+    hop(2, 5)
+    hop(3, 3)
+    far(0)
+    hop(4, 1)
+    hop(2, 6)
+    hop(4, 2)
+    own(2)
+    hop(3, 4)
+    far(1)
+    hop(2, 7)
+    hop(3, 5)
+    own(3)
+    hop(4, 3)
+    hop(3, 6)
+    far(2)
+    hop(3, 7)
+    own(4)
+    hop(4, 4, 5)
+    own(5)
+    hop(4, 6, 7)
     for k in range(1, SPANS):
         y_copy(k).wait_send()
-    for way, d, k in sent:
+    early, late = sent[:-16], sent[-16:]
+    for way, d, k in early:
+        z_copy(way, d, k).wait_send()
+    far(3)
+    own(6)
+    own(7)
+    for p in (4, 5, 6, 7):
+        far(p)
+    for way, d, k in late:
         z_copy(way, d, k).wait_send()
 
 
@@ -297,7 +332,8 @@
             pltpu.VMEM((DEPTH, 2 * WIDTH), BF16),
             pltpu.VMEM((1, DEPTH), F32),
             pltpu.VMEM((2, 64, 128), BF16),
-            pltpu.VMEM((256, WIDTH), F32),
+            pltpu.VMEM((512, WIDTH), F32),
+            pltpu.VMEM((256, DEPTH), BF16),
             pltpu.SemaphoreType.DMA((12,)),
             pltpu.SemaphoreType.DMA((SPANS,)),
             pltpu.SemaphoreType.DMA((SPANS,)),

time: 73 us -> 67.7 us (0.927)
  Pallas kernels: 72.3 us -> 66.3 us
    pallas_call x1, Pallas kernels: 69.9 us -> 63.9 us  [shards(): pl.pallas_call(exchange_kernel, out_shape=(pltpu.VMEM((2, WIDTH + TURN, l...]
where the time goes in v2:
time: 67.7 us; the launch traced here: 66.9 us
  Pallas kernels  66.3 us (98%)
    pallas_call x1, Pallas kernels, shards(): pl.pallas_call(exchange_kernel, out_shape=(pltpu.VMEM((2, WIDTH + TURN, l...  63.9 us
    pallas_call x1, Pallas kernels, shards(): pl.pallas_call(write_kernel, out_shape=(jax.ShapeDtypeStruct((1, 2, WIDTH...  2.4 us

profile of v2, /device:TPU:1, one launch (start us, length us, event | category | flops | bytes accessed | tf_op | source)
XLA Modules:
  0.0 66.9 jit_solution(14399208359149716308)
XLA Ops:
  0.6 63.9 %shard_map.68 = (bf16[2,192,4096]{2,1,0:T(8,128)(2,1)S(1)}, bf16[8192,128]{1,0:T(8,128)(2,1)S(1)}) custom-call(bf16[16,32,512]{2,1,0:T(8,128)(2,1)} %lat.1, bf16[16,32,64]{2,1,0:T(8,128)(2,1)} %rot.1, f32[1,512]{1,0:T(1,128)} %bitcast.6, bf16[1024,128]{1,0:T(8,128)(2,1)} %bitcast.4, bf16[1024,128]{1,0:T(8,128)(2,1)} %bitcast.5), custom_call_target="tpu_custom_call" | custom-call | tf_op jit(solution)/shard_map/pallas_call | solution.py:318
  64.5 2.4 %shard_map.69 = (bf16[1,2,192,4096]{3,2,1,0:T(8,128)(2,1)}, bf16[8192,128]{1,0:T(8,128)(2,1)}) custom-call(bf16[2,192,4096]{2,1,0:T(8,128)(2,1)S(1)} %get-tuple-element.6.keys_part, bf16[8192,128]{1,0:T(8,128)(2,1)S(1)} %get-tuple-element.7.values_part), custom_call_target="tpu_custom_call" | custom-call | tf_op jit(solution)/shard_map/pallas_call | solution.py:347

commit v3 on v2

v3 whole, which is shorter than its diff:
```python
import functools

import jax
import jax.numpy as jnp
from jax import lax
from jax.experimental import pallas as pl
from jax.experimental.pallas import tpu as pltpu
from jax.sharding import PartitionSpec as P

MESH = pl.DeviceIdType.MESH
BF16, F32 = jnp.bfloat16, jnp.float32

SPANS, RING = 16, 8
COUNT, DEPTH = 32, 512
TURN, WIDTH = 64, 128
NEAR = 6
LAST = 7
TILES = 8


def widen_rows(rows, rotary, key_up, value_up):
    wide_keys = jnp.einsum(
        "btr,rhk->bthk", rows, key_up, preferred_element_type=jnp.float32
    ).astype(jnp.bfloat16)
    shared = jnp.broadcast_to(rotary[:, :, None], wide_keys.shape[:3] + rotary.shape[2:])
    wide_values = jnp.einsum(
        "btr,rhk->bthk", rows, value_up, preferred_element_type=jnp.float32
    ).astype(jnp.bfloat16)
    return (jnp.concatenate([wide_keys, shared], axis=-1), wide_values)


def unit_rows(vectors, row_gain):
    return (
        vectors * lax.rsqrt(jnp.mean(vectors * vectors, axis=-1, keepdims=True) + 1e-06) * row_gain
    )


def plain_shards(latents, rotary_rows, latent_gain, key_up, value_up):
    rows_ready = unit_rows(latents.astype(jnp.float32), latent_gain).astype(jnp.bfloat16)

    def move(block):
        block = lax.all_to_all(block, "span", split_axis=0, concat_axis=1, tiled=True)
        block = block.reshape(block.shape[0], lax.axis_size("span"), -1, block.shape[2])
        block = lax.all_gather(block, "heads", axis=2, tiled=True)
        return block.reshape(block.shape[0], -1, block.shape[3])

    cache_keys, cache_values = widen_rows(move(rows_ready), move(rotary_rows), key_up, value_up)
    return (jnp.transpose(cache_keys, (0, 2, 3, 1)), cache_values)


def source(me, k):
    j, flip = k // 2, k % 2
    away = ((j + 1) // 2) * (2 * (j % 2) - 1)
    core = (me % 2) * (1 - 2 * flip) + flip
    return ((me // 2 + away + SPANS // 2) % (SPANS // 2)) * 2 + core


def target(me, k):
    j, flip = k // 2, k % 2
    away = ((j + 1) // 2) * (2 * (j % 2) - 1)
    core = (me % 2) * (1 - 2 * flip) + flip
    return ((me // 2 - away + SPANS // 2) % (SPANS // 2)) * 2 + core


def y_unit(k):
    return (k,) if k < NEAR else (k // 2 * 2, k // 2 * 2 + 1)


def z_unit(d, k):
    return (k,) if (d == 1 and k < NEAR) or (d == 2 and k < 2) else (k // 2 * 2, k // 2 * 2 + 1)


def last_way(k):
    return k // 2 % 2


Y_SEMS, Z_SEMS = {}, {}
for place in range(SPANS):
    Y_SEMS[place] = len({y_unit(k) for k in range(1, place + 1)}) - 1
for way, hops, place in [(w, d, k) for w in range(2) for d in range(1, 5) for k in range(SPANS)]:
    if z_unit(hops, place)[0] == place and (hops < 4 or way == last_way(place)):
        Z_SEMS[way, hops, place] = len(Z_SEMS)


def expand_pair(tile, key_wide, value_wide, gain, pick, ready, flat, put_keys, put_values):
    for i in range(2):
        for zz in range(4):
            for half in range(2):
                raw = jnp.concatenate(
                    [tile(i, zz, half * 4 + c).astype(F32) for c in range(4)], axis=1
                )
                ready[pl.ds(i * 128 + zz * 32 + half * 16, 16), :] = (
                    unit_rows(raw, gain[...]).astype(BF16)
                )
    wide = lax.dot_general(
        key_wide[...], ready[...], (((1,), (1,)), ((), ())), preferred_element_type=F32
    ).astype(BF16)
    for i in range(2):
        turned = jnp.concatenate([tile(i, zz, TILES) for zz in range(4)], axis=0)
        halves = [
            lax.dot_general(
                turned, pick[half], (((0,), (0,)), ((), ())), preferred_element_type=F32
            )
            for half in range(2)
        ]
        shared = (halves[0][:TURN] + halves[1][TURN:]).astype(BF16)
        for h in range(2):
            put_keys(i, h, 0, wide[h * WIDTH:(h + 1) * WIDTH, i * 128:(i + 1) * 128])
            put_keys(i, h, WIDTH, shared)
    wide = jnp.dot(ready[...], value_wide[...], preferred_element_type=F32)
    for h in range(2):
        flat[pl.ds(h, 256, stride=2), :] = wide[:, h * WIDTH:(h + 1) * WIDTH]
    for i in range(2):
        put_values(i, flat[pl.ds(i * 256, 256), :].astype(BF16))


def exchange_kernel(
    lat, rot, far_gain, key_up, value_up, keys, values, late, key_wide, value_wide, gain, pick,
    buf, stage, rot_raw, raw_w, flat,
    ready, load_sem, y_send, y_recv, z_send, z_recv, round_sem,
):
    me, z = lax.axis_index("span"), lax.axis_index("heads")
    ahead, behind = lax.rem(z + 1, RING), lax.rem(z + RING - 1, RING)

    sibling = target(me, 1)

    rot_load = pltpu.make_async_copy(rot, rot_raw, load_sem.at[0])
    rot_load.start()
    for t in range(TILES):
        rows = pl.ds(16 * (t // 4), 16)
        columns = pl.ds(128 * (t % 4), 128)
        pltpu.make_async_copy(
            lat.at[:, rows, columns], stage.at[:, t], load_sem.at[1]
        ).start()
    gain_load = pltpu.make_async_copy(far_gain, gain, load_sem.at[2])
    gain_load.start()
    for w, weight in enumerate((key_up, value_up)):
        pltpu.make_async_copy(weight, raw_w.at[w], load_sem.at[3]).start()

    barrier = pltpu.get_barrier_semaphore()
    greeted = [{"heads": near} for near in (ahead, behind)] + [{"span": target(me, k)} for k in range(1, NEAR)]
    greeted += [{"span": sibling, "heads": near} for near in (ahead, behind)]
    for device in greeted:
        pl.semaphore_signal(barrier, inc=1, device_id=device, device_id_type=MESH)

    rot_load.wait()
    for s in range(SPANS):
        part = rot_raw[s].astype(F32)
        stage[s, TILES] = jnp.concatenate([part[:16], part[16:]], axis=1).astype(BF16)

    all_rows = stage.at[:, pl.ds(0, TILES)]
    pltpu.make_async_copy(all_rows, all_rows, load_sem.at[1]).wait()
    pl.semaphore_wait(barrier, len(greeted))
    for near in (ahead, behind):
        pl.semaphore_signal(round_sem, inc=1, device_id={"heads": near}, device_id_type=MESH)

    def z_copy(way, d, ks):
        if way == 0:
            here, there, to = (RING + 1 - d) % RING, RING - d, ahead
        else:
            here, there, to = d - 1, d, behind
        places = pl.ds(ks[0], len(ks))
        src, device = buf.at[here, places], {"heads": to}
        if d == 1 and ks == (0,):
            src = stage.at[pl.ds(me, 1)]
        elif d == 1 and ks[0] < NEAR:
            to_span = target(me, ks[0])
            src, device = stage.at[pl.ds(to_span, 1)], {"span": to_span, "heads": to}
        return pltpu.make_async_remote_copy(
            src_ref=src, dst_ref=buf.at[there, places],
            send_sem=z_send.at[0], recv_sem=z_recv.at[Z_SEMS[way, d, ks[0]]],
            device_id=device, device_id_type=MESH,
        )

    def y_copy(k):
        to = target(me, k)
        return pltpu.make_async_remote_copy(
            src_ref=stage.at[pl.ds(to, 1)], dst_ref=buf.at[0, pl.ds(k, 1)],
            send_sem=y_send.at[0], recv_sem=y_recv.at[Y_SEMS[k]],
            device_id={"span": to}, device_id_type=MESH,
        )

    heard = set()

    def need(way, d, k):
        if d == 0:
            ks = y_unit(k)
            if ks != (0,) and (0, ks) not in heard:
                heard.add((0, ks))
                places = buf.at[0, pl.ds(ks[0], len(ks))]
                pltpu.make_async_remote_copy(
                    src_ref=places, dst_ref=places, send_sem=y_send.at[0],
                    recv_sem=y_recv.at[Y_SEMS[ks[0]]],
                    device_id={"span": sibling}, device_id_type=MESH,
                ).wait_recv()
            return
        ks = z_unit(d, k)
        if (way, d, ks) not in heard:
            heard.add((way, d, ks))
            z_copy(way, d, ks).wait_recv()

    def forward(d, ks):
        for unit in dict.fromkeys(z_unit(d, k) for k in ks):
            for way in (0, 1):
                if d > 1 or unit[0] >= NEAR:
                    for k in unit:
                        need(way, d - 1, k)
                if d < 4 or way == last_way(unit[0]):
                    z_copy(way, d, unit).start()

    def spread(ks):
        for k in ks:
            y_copy(k).start()

    forward(1, [0, 1])
    spread(range(1, NEAR))
    buf[0, 0] = stage[me]

    gain_load.wait()
    pltpu.make_async_copy(raw_w, raw_w, load_sem.at[3]).wait()
    for w, put in ((0, key_wide), (1, value_wide)):
        @pl.loop(0, 4)
        def _(n):
            r = pl.multiple_of(n * 256, 256)
            flat[pl.ds(0, 256), :] = raw_w[w, pl.ds(r, 256), :].astype(F32)
            at = pl.multiple_of(n * 128, 128)
            for h in range(2):
                block = flat[pl.ds(h, 128, stride=2), :]
                if w == 0:
                    key_wide[h * WIDTH:(h + 1) * WIDTH, pl.ds(at, 128)] = block.T.astype(BF16)
                else:
                    value_wide[pl.ds(at, 128), h * WIDTH:(h + 1) * WIDTH] = block.astype(BF16)
    row = lax.broadcasted_iota(jnp.int32, (64, 128), 0)
    column = lax.broadcasted_iota(jnp.int32, (64, 128), 1)
    for half in range(2):
        place = (row // 16) * 32 + half * 16 + row % 16
        pick[half] = jnp.where(place == column, 1.0, 0.0).astype(BF16)

    def expand(p, other):
        group = z // 4 if not other else 1 - z // 4
        pair = (2 * p, 2 * p + 1)
        for k in pair:
            need(0, 0, k)
            for way in (0, 1):
                need(way, 3, k)
            if other:
                need(last_way(k), 4, k)
        rels = [lax.rem(group * 4 + zz + RING - z, RING) for zz in range(4)]
        if other and p == LAST:
            for i, k in enumerate(pair):
                for zz in range(4):
                    late[i, zz] = buf[rels[zz], k]
            return
        starts = [pl.multiple_of(source(me, k) * 256 + group * 128, 128) for k in pair]

        def put_keys(i, h, first, block):
            keys[h, first:first + block.shape[0], pl.ds(starts[i], 128)] = block

        def put_values(i, block):
            values[pl.ds(pl.multiple_of(starts[i] * 2, 256), 256), :] = block

        expand_pair(
            lambda i, zz, t: buf[rels[zz], pair[i], t],
            key_wide, value_wide, gain, pick, ready, flat, put_keys, put_values,
        )

    def hop(d, *pairs):
        for p in pairs:
            forward(d, [2 * p, 2 * p + 1])

    own, far = functools.partial(expand, other=False), functools.partial(expand, other=True)

    pl.semaphore_wait(round_sem, 2)
    forward(1, range(2, NEAR))
    forward(2, [0])
    for k in range(2, NEAR):
        need(0, 0, k)
    spread(range(NEAR, 10))
    forward(2, [1])
    hop(2, 1, 2)
    hop(1, 3, 4)
    spread(range(10, 16))
    hop(3, 0)
    hop(2, 3, 4)
    hop(1, 5, 6)
    hop(3, 1)
    hop(2, 5)
    own(0)
    hop(2, 6)
    hop(1, 7)
    hop(3, 2)
    hop(3, 3)
    own(1)
    hop(2, 7)
    hop(3, 4)
    own(2)
    hop(4, 0, 1)
    own(3)
    hop(3, 5)
    hop(3, 6)
    far(0)
    hop(3, 7)
    own(4)
    hop(4, 2, 3)
    far(1)
    own(5)
    hop(4, 4, 5)
    own(6)
    hop(4, 6, 7)
    own(7)
    for p in range(2, 8):
        far(p)
    for held, sem in ((buf.at[pl.ds(0, RING - 1)], z_send), (stage.at[pl.ds(0, SPANS - 1)], y_send)):
        pltpu.make_async_remote_copy(
            src_ref=held, dst_ref=held, send_sem=sem.at[0], recv_sem=y_recv.at[0],
            device_id={"span": sibling}, device_id_type=MESH,
        ).wait_send()


def write_kernel(
    keys_part, values_part, late, key_wide, value_wide, gain, pick, keys, values,
    ready, flat, keys_late, values_late, sem,
):
    me, z = lax.axis_index("span"), lax.axis_index("heads")
    near, away = z // 4, 1 - z // 4
    for k in range(SPANS):
        first, size = source(me, k) * 256, 256
        if k // 2 == LAST:
            first, size = first + near * 128, 128
        columns = pl.ds(pl.multiple_of(first, 128), size)
        rows = pl.ds(pl.multiple_of(first * 2, 256), size * 2)
        pltpu.make_async_copy(keys_part.at[:, :, columns], keys.at[0, :, :, columns], sem.at[0]).start()
        pltpu.make_async_copy(values_part.at[rows], values.at[rows], sem.at[1]).start()

    def put_keys(i, h, first, block):
        keys_late[i, h, first:first + block.shape[0], :] = block

    def put_values(i, block):
        values_late[i] = block

    expand_pair(
        lambda i, zz, t: late[i, zz, t],
        key_wide, value_wide, gain, pick, ready, flat, put_keys, put_values,
    )
    for i in range(2):
        first = source(me, 2 * LAST + i) * 256 + away * 128
        columns = pl.ds(pl.multiple_of(first, 128), 128)
        rows = pl.ds(pl.multiple_of(first * 2, 256), 256)
        pltpu.make_async_copy(keys_late.at[i], keys.at[0, :, :, columns], sem.at[2]).start()
        pltpu.make_async_copy(values_late.at[i], values.at[rows], sem.at[3]).start()
    length = keys_part.shape[2]
    early = (keys_part.at[:, :, pl.ds(0, length - 256)], values_part.at[pl.ds(0, 2 * length - 512)])
    for n, held in enumerate((*early, keys_late, values_late)):
        pltpu.make_async_copy(held, held, sem.at[n]).wait()


def shards(latents, rotary_rows, latent_gain, key_up, value_up):
    shape = (lax.axis_size("span"), lax.axis_size("heads"), *latents.shape, rotary_rows.shape[2])
    if shape != (SPANS, RING, SPANS, COUNT, DEPTH, TURN) or key_up.shape != (DEPTH, 2, WIDTH) or (
        value_up.shape != (DEPTH, 2, WIDTH)
    ):
        return plain_shards(latents, rotary_rows, latent_gain, key_up, value_up)
    length = SPANS * RING * COUNT
    near = pl.BlockSpec(memory_space=pltpu.VMEM)
    far = pl.BlockSpec(memory_space=pltpu.HBM)
    args = (
        latents, rotary_rows, latent_gain[None],
        key_up.reshape(2 * DEPTH, WIDTH), value_up.reshape(2 * DEPTH, WIDTH),
    )
    parts = pl.pallas_call(
        exchange_kernel,
        out_shape=(
            pltpu.VMEM((2, WIDTH + TURN, length), BF16),
            pltpu.VMEM((2 * length, WIDTH), BF16),
            pltpu.VMEM((2, 4, TILES + 1, 16, 128), BF16),
            pltpu.VMEM((2 * WIDTH, DEPTH), BF16),
            pltpu.VMEM((DEPTH, 2 * WIDTH), BF16),
            pltpu.VMEM((1, DEPTH), F32),
            pltpu.VMEM((2, 64, 128), BF16),
        ),
        in_specs=[far] * 5,
        out_specs=[near] * 7,
        scratch_shapes=[
            pltpu.VMEM((RING, SPANS, TILES + 1, 16, 128), BF16),
            pltpu.VMEM((SPANS, TILES + 1, 16, 128), BF16),
            pltpu.VMEM((SPANS, COUNT, TURN), BF16),
            pltpu.VMEM((2, 2 * DEPTH, WIDTH), BF16),
            pltpu.VMEM((512, WIDTH), F32),
            pltpu.VMEM((256, DEPTH), BF16),
            pltpu.SemaphoreType.DMA((4,)),
            pltpu.SemaphoreType.DMA((1,)),
            pltpu.SemaphoreType.DMA((Y_SEMS[SPANS - 1] + 1,)),
            pltpu.SemaphoreType.DMA((1,)),
            pltpu.SemaphoreType.DMA((len(Z_SEMS),)),
            pltpu.SemaphoreType.REGULAR,
        ],
        compiler_params=pltpu.CompilerParams(
            collective_id=0, has_side_effects=True, vmem_limit_bytes=40 * 1024 * 1024
        ),
    )(*(pltpu.with_memory_space_constraint(arg, pltpu.HBM) for arg in args))
    keys, values = pl.pallas_call(
        write_kernel,
        out_shape=(
            jax.ShapeDtypeStruct((1, 2, WIDTH + TURN, length), BF16),
            jax.ShapeDtypeStruct((2 * length, WIDTH), BF16),
        ),
        in_specs=[near] * 7,
        out_specs=[far] * 2,
        scratch_shapes=[
            pltpu.VMEM((256, DEPTH), BF16),
            pltpu.VMEM((512, WIDTH), F32),
            pltpu.VMEM((2, 2, WIDTH + TURN, 128), BF16),
            pltpu.VMEM((2, 256, WIDTH), BF16),
            pltpu.SemaphoreType.DMA((4,)),
        ],
        compiler_params=pltpu.CompilerParams(vmem_limit_bytes=16 * 1024 * 1024),
    )(*parts)
    return keys, values.reshape(1, length, 2, WIDTH)


def solution(mesh):
    return jax.shard_map(
        shards,
        mesh=mesh,
        in_specs=(
            P("trial", ("span", "heads"), None),
            P("trial", ("span", "heads"), None),
            P(),
            P("trial", "heads", None),
            P("trial", "heads", None),
        ),
        out_specs=(
            P(("trial", "span"), "heads", None, None),
            P(("trial", "span"), None, "heads", None),
        ),
        check_vma=False,
    )
```

time: 67.7 us -> 65.6 us (0.969); the launches traced: 66.9 us -> 65.5 us
  Pallas kernels: 66.3 us -> 64.9 us
    pallas_call x1, Pallas kernels: 63.9 us -> 62.2 us  [shards(): pl.pallas_call(exchange_kernel, out_shape=(pltpu.VMEM((2, WIDTH + TURN, l...]
where the time goes in v3:
time: 65.6 us; the launch traced here: 65.5 us
  Pallas kernels  64.9 us (99%)
    pallas_call x1, Pallas kernels, shards(): pl.pallas_call(exchange_kernel, out_shape=(pltpu.VMEM((2, WIDTH + TURN, l...  62.2 us
    pallas_call x1, Pallas kernels, shards(): pl.pallas_call(write_kernel, out_shape=(jax.ShapeDtypeStruct((1, 2, WIDTH...  2.65 us

profile of v3, /device:TPU:1, one launch (start us, length us, event | category | flops | bytes accessed | tf_op | source)
XLA Modules:
  0.0 65.5 jit_solution(4213048111525514769)
XLA Ops:
  0.6 62.2 %shard_map.68 = (bf16[2,192,4096]{2,1,0:T(8,128)(2,1)S(1)}, bf16[8192,128]{1,0:T(8,128)(2,1)S(1)}, bf16[2,4,9,16,128]{4,3,2,1,0:T(8,128)(2,1)S(1)}, bf16[256,512...) custom-call(bf16[16,32,512]{2,1,0:T(8,128)(2,1)} %lat.1, ...), custom_call_target="tpu_custom_call" | custom-call | tf_op jit(solution)/shard_map/pallas_call | solution.py:370
  62.8 2.7 %shard_map.69 = (bf16[1,2,192,4096]{3,2,1,0:T(8,128)(2,1)}, bf16[8192,128]{1,0:T(8,128)(2,1)}) custom-call(bf16[2,192,4096]{2,1,0:T(8,128)(2,1)S(1)} %get-tuple-element.11.keys_part, bf16[8192,128]{1,0:T(8,128)(2,1)S(1)} %get-tuple-element.12.values_part, bf16[2,4,9,16,128]{4,3,2,1,0:T(8,128)(2,1)S(1)} %get-tuple-element.13.late, ...), custom_call_target="tpu_custom_call" | custom-call | tf_op jit(solution)/shard_map/pallas_call | solution.py:401

commit v4 on v3

--- a/solution.py
+++ b/solution.py
@@ -67,11 +67,12 @@
 
 
 def z_unit(d, k):
-    return (k,) if (d == 1 and k < NEAR) or (d == 2 and k < 2) else (k // 2 * 2, k // 2 * 2 + 1)
+    alone = (d == 1 and k < NEAR) or (d == 2 and k < 2) or d == 4
+    return (k,) if alone else (k // 2 * 2, k // 2 * 2 + 1)
 
 
 def last_way(k):
-    return k // 2 % 2
+    return k % 2
 
 
 Y_SEMS, Z_SEMS = {}, {}
@@ -282,8 +283,8 @@
     spread(range(10, 16))
     hop(3, 0)
     hop(2, 3, 4)
+    hop(3, 1)
     hop(1, 5, 6)
-    hop(3, 1)
     hop(2, 5)
     own(0)
     hop(2, 6)
@@ -293,20 +294,20 @@
     own(1)
     hop(2, 7)
     hop(3, 4)
+    hop(4, 0, 1)
     own(2)
-    hop(4, 0, 1)
-    own(3)
     hop(3, 5)
     hop(3, 6)
+    own(3)
+    hop(3, 7)
+    hop(4, 2, 3)
+    own(4)
     far(0)
-    hop(3, 7)
-    own(4)
-    hop(4, 2, 3)
     far(1)
+    hop(4, 4, 5)
     own(5)
-    hop(4, 4, 5)
+    hop(4, 6, 7)
     own(6)
-    hop(4, 6, 7)
     own(7)
     for p in range(2, 8):
         far(p)

time: 65.6 us -> 64.4 us (0.982)
  Pallas kernels: 64.9 us -> 63.2 us
    pallas_call x1, Pallas kernels: 62.2 us -> 60.5 us  [shards(): pl.pallas_call(exchange_kernel, out_shape=(pltpu.VMEM((2, WIDTH + TURN, l...]
where the time goes in v4:
time: 64.4 us; the launch traced here: 63.8 us
  Pallas kernels  63.2 us (98%)
    pallas_call x1, Pallas kernels, shards(): pl.pallas_call(exchange_kernel, out_shape=(pltpu.VMEM((2, WIDTH + TURN, l...  60.5 us
    pallas_call x1, Pallas kernels, shards(): pl.pallas_call(write_kernel, out_shape=(jax.ShapeDtypeStruct((1, 2, WIDTH...  2.65 us

profile of v4, /device:TPU:1, one launch (start us, length us, event | category | flops | bytes accessed | tf_op | source)
XLA Modules:
  0.0 63.8 jit_solution(13249424084839025594)
XLA Ops:
  0.6 60.5 %shard_map.68 = (bf16[2,192,4096]{2,1,0:T(8,128)(2,1)S(1)}, bf16[8192,128]{1,0:T(8,128)(2,1)S(1)}, bf16[2,4,9,16,128]{4,3,2,1,0:T(8,128)(2,1)S(1)}, bf16[256,512...) custom-call(bf16[16,32,512]{2,1,0:T(8,128)(2,1)} %lat.1, ...), custom_call_target="tpu_custom_call" | custom-call | tf_op jit(solution)/shard_map/pallas_call | solution.py:371
  61.2 2.7 %shard_map.69 = (bf16[1,2,192,4096]{3,2,1,0:T(8,128)(2,1)}, bf16[8192,128]{1,0:T(8,128)(2,1)}) custom-call(bf16[2,192,4096]{2,1,0:T(8,128)(2,1)S(1)} %get-tuple-element.11.keys_part, bf16[8192,128]{1,0:T(8,128)(2,1)S(1)} %get-tuple-element.12.values_part, bf16[2,4,9,16,128]{4,3,2,1,0:T(8,128)(2,1)S(1)} %get-tuple-element.13.late, ...), custom_call_target="tpu_custom_call" | custom-call | tf_op jit(solution)/shard_map/pallas_call | solution.py:402

commit v5 on v4

--- a/solution.py
+++ b/solution.py
@@ -71,6 +71,10 @@
     return (k,) if alone else (k // 2 * 2, k // 2 * 2 + 1)
 
 
+def wait_unit(d, k):
+    return z_unit(d, k) if d < 3 and k < 2 else (k // 2 * 2, k // 2 * 2 + 1)
+
+
 def last_way(k):
     return k % 2
 
@@ -79,8 +83,8 @@
 for place in range(SPANS):
     Y_SEMS[place] = len({y_unit(k) for k in range(1, place + 1)}) - 1
 for way, hops, place in [(w, d, k) for w in range(2) for d in range(1, 5) for k in range(SPANS)]:
-    if z_unit(hops, place)[0] == place and (hops < 4 or way == last_way(place)):
-        Z_SEMS[way, hops, place] = len(Z_SEMS)
+    first = (0 if hops == 4 else way, hops, wait_unit(hops, place)[0])
+    Z_SEMS[way, hops, place] = Z_SEMS.setdefault(first, len(set(Z_SEMS.values())))
 
 
 def expand_pair(tile, key_wide, value_wide, gain, pick, ready, flat, put_keys, put_values):
@@ -195,10 +199,16 @@
                     device_id={"span": sibling}, device_id_type=MESH,
                 ).wait_recv()
             return
-        ks = z_unit(d, k)
-        if (way, d, ks) not in heard:
-            heard.add((way, d, ks))
-            z_copy(way, d, ks).wait_recv()
+        ks = wait_unit(d, k)
+        mark = (None if d == 4 else way, d, ks)
+        if mark not in heard:
+            heard.add(mark)
+            places = buf.at[d if way else RING - d, pl.ds(ks[0], len(ks))]
+            pltpu.make_async_remote_copy(
+                src_ref=places, dst_ref=places, send_sem=z_send.at[0],
+                recv_sem=z_recv.at[Z_SEMS[way, d, k]],
+                device_id={"heads": ahead}, device_id_type=MESH,
+            ).wait_recv()
 
     def forward(d, ks):
         for unit in dict.fromkeys(z_unit(d, k) for k in ks):
@@ -392,7 +402,7 @@
             pltpu.SemaphoreType.DMA((1,)),
             pltpu.SemaphoreType.DMA((Y_SEMS[SPANS - 1] + 1,)),
             pltpu.SemaphoreType.DMA((1,)),
-            pltpu.SemaphoreType.DMA((len(Z_SEMS),)),
+            pltpu.SemaphoreType.DMA((len(set(Z_SEMS.values())),)),
             pltpu.SemaphoreType.REGULAR,
         ],
         compiler_params=pltpu.CompilerParams(

time: 64.4 us -> 64.3 us (level)
  no operation moved by 1% of the time
where the time goes in v5:
time: 64.3 us; the launch traced here: 63.7 us
  Pallas kernels  63.1 us (98%)
    pallas_call x1, Pallas kernels, shards(): pl.pallas_call(exchange_kernel, out_shape=(pltpu.VMEM((2, WIDTH + TURN, l...  60.4 us
    pallas_call x1, Pallas kernels, shards(): pl.pallas_call(write_kernel, out_shape=(jax.ShapeDtypeStruct((1, 2, WIDTH...  2.65 us

profile of v5, /device:TPU:1, one launch (start us, length us, event | category | flops | bytes accessed | tf_op | source)
XLA Modules:
  0.0 63.7 jit_solution(13169871110586047147)
XLA Ops:
  0.6 60.4 %shard_map.68 = (bf16[2,192,4096]{2,1,0:T(8,128)(2,1)S(1)}, bf16[8192,128]{1,0:T(8,128)(2,1)S(1)}, bf16[2,4,9,16,128]{4,3,2,1,0:T(8,128)(2,1)S(1)}, bf16[256,512...) custom-call(bf16[16,32,512]{2,1,0:T(8,128)(2,1)} %lat.1, ...), custom_call_target="tpu_custom_call" | custom-call | tf_op jit(solution)/shard_map/pallas_call | solution.py:381
  61.0 2.7 %shard_map.69 = (bf16[1,2,192,4096]{3,2,1,0:T(8,128)(2,1)}, bf16[8192,128]{1,0:T(8,128)(2,1)}) custom-call(bf16[2,192,4096]{2,1,0:T(8,128)(2,1)S(1)} %get-tuple-element.11.keys_part, bf16[8192,128]{1,0:T(8,128)(2,1)S(1)} %get-tuple-element.12.values_part, bf16[2,4,9,16,128]{4,3,2,1,0:T(8,128)(2,1)S(1)} %get-tuple-element.13.late, ...), custom_call_target="tpu_custom_call" | custom-call | tf_op jit(solution)/shard_map/pallas_call | solution.py:412
